TPU v7x, 32 devices: a whole 2x2x4 slice. The times are simulated.
32 devices in a mesh: replica: 16 (over z, x, core), spatial: 2 (over y).
Axes of the slice: x: 2, y: 2, z: 4, core: 2. Of those that a mesh axis runs over, the one named last changes fastest.
Arguments:
- grads: bfloat16 [16, 2, 852992], P('replica', 'spatial'), may hold values from -6 to 6
- master: float32 [852992], P(('replica', 'spatial')), may hold values from -0.06 to 0.06
- velocity: float32 [852992], P(('replica', 'spatial')), may hold values from -0.3 to 0.3
- layer_offsets: int32 [6], replicated, may hold values from 0 to 852736, as said below
- layer_sizes: int32 [6], replicated, may hold values from 256 to 589824
- lars_skip: int32 [6], replicated, may hold values from 0 to 1
Outputs:
- new_weights: bfloat16 [852992], replicated
- new_master: float32 [852992], P(('replica', 'spatial'))
- new_velocity: float32 [852992], P(('replica', 'spatial'))
Inputs may be any that keep to these rules, and one draw needn't show every extreme that they name: layer_offsets, layer_sizes and lars_skip describe the six tensors (a 256 x 1024 convolution, a 256 x 256 x 9 convolution, and two gains and two shifts of 256 entries) laid end to end in some order without gaps, the last of them always a gain or a shift; lars_skip is 1 exactly for the gains and shifts.
All inputs are finite; a program needn't handle non-finite values.
Results may differ from a plain program's by a relative error of at most 0.001.
Values may be sent and summed in bfloat16 or wider, within the bound.
A program may use at most 64 MiB of HBM per device.

v0:
```python
import jax
import jax.numpy as jnp
from jax import lax
from jax.sharding import PartitionSpec as P


def shards(grads, master, velocity, layer_offsets, layer_sizes, lars_skip):
    n_rep = lax.axis_size("replica")
    n_spa = lax.axis_size("spatial")
    shard = master.shape[0]
    position = lax.axis_index(("replica", "spatial")) * shard + jnp.arange(shard, dtype=jnp.int32)
    inside = (position[None, :] >= layer_offsets[:, None]) & (
        position[None, :] < (layer_offsets + layer_sizes)[:, None]
    )
    onehot = inside.astype(jnp.float32)
    received = lax.all_to_all(
        grads[0, 0].reshape(n_rep, n_spa * shard),
        "replica",
        split_axis=0,
        concat_axis=0,
        tiled=True,
    )
    first = jnp.sum(received.astype(jnp.float32), axis=0)
    summed = lax.psum_scatter(
        first.reshape(n_spa, shard), "spatial", scatter_dimension=0, tiled=True
    )
    grad = summed.reshape(shard) / (n_rep * n_spa)
    gsq_local = jnp.dot(onehot, grad * grad, precision=lax.Precision.HIGHEST)
    wsq_local = jnp.dot(onehot, master * master, precision=lax.Precision.HIGHEST)
    wsq, gsq = lax.psum((wsq_local, gsq_local), ("replica", "spatial"))
    wnorm = jnp.sqrt(wsq)
    gnorm = jnp.sqrt(gsq)
    skipped = lars_skip.astype(jnp.float32)
    ratio = 0.02 * wnorm / (gnorm + 0.001 * wnorm + 1e-06)
    trust = skipped + (1.0 - skipped) * ratio
    decay = (1.0 - skipped) * 0.001
    trust_pos = jnp.dot(trust, onehot, precision=lax.Precision.HIGHEST)
    decay_pos = jnp.dot(decay, onehot, precision=lax.Precision.HIGHEST)
    new_velocity = 0.9 * velocity + 8.0 * trust_pos * (grad + decay_pos * master)
    new_master = master - new_velocity
    new_weights = lax.all_gather(
        new_master.astype(jnp.bfloat16), ("replica", "spatial"), axis=0, tiled=True
    )
    return (new_weights, new_master, new_velocity)


def solution(mesh):
    return jax.shard_map(
        shards,
        mesh=mesh,
        in_specs=(
            P("replica", "spatial", None),
            P(("replica", "spatial")),
            P(("replica", "spatial")),
            P(),
            P(),
            P(),
        ),
        out_specs=(P(), P(("replica", "spatial")), P(("replica", "spatial"))),
        check_vma=False,
    )
```

profile of v0, /device:TPU:0, one launch (start us, length us, event | category | flops | bytes accessed | tf_op | source)
XLA Modules:
  0.0 341.0 jit_solution(4959349934665128111)
XLA Ops:
  7.2 37.8 %reduce.1 = bf16[852992]{0:T(1024)(128)(2,1)} reduce(bf16[1,1,852992]{2,1,0:T(2,128)(2,1)} %param.6, bf16[]{:T(256)} %constant.38), dimensions={0,1}, to_apply=%param.6.reduce_sub_computation | reduce | bytes 3411970 | tf_op args[0]
  44.9 3.0 all_to_all.8
  48.4 13.3 %reduce.8 = bf16[16,53312]{1,0:T(8,128)(2,1)} reduce(bf16[16,1,53312]{2,1,0:T(2,128)(2,1)S(1)} %all_to_all.8, bf16[]{:T(256)} %broadcast.54), dimensions={1}, to_apply=%all_to_all.8.reduce_sub_computation | reduce | bytes 3411970 | tf_op jit(solution)/shard_map/all_to_all | solution.py:16
  61.8 3.2 reshape.38
  65.0 7.6 %all-to-all-start = ((bf16[16,2,26656]{2,1,0:T(2,128)(2,1)}), bf16[16,2,26656]{2,1,0:T(2,128)(2,1)}, u32[]{:S(2)}, u32[]{:S(2)}) async-start(bf16[16,2,26656]{2,1,0:T(2,128)(2,1)} %reshape.38), calls=%async_computation | async-start | bytes 3424256 | tf_op jit(solution)/shard_map/all_to_all | solution.py:16
  72.6 0.7 reshape.25
  73.4 0.7 dynamic-slice
  74.1 0.7 iota_add_fusion
  74.7 32.2 %all-to-all-done = bf16[16,2,26656]{2,1,0:T(2,128)(2,1)} async-done(((bf16[16,2,26656]{2,1,0:T(2,128)(2,1)}), bf16[16,2,26656]{2,1,0:T(2,128)(2,1)}, u32[]{:S(2)}, u32[]{:S(2)}) %all-to-all-start) | async-done | bytes 1706016 | tf_op jit(solution)/shard_map/all_to_all | solution.py:16
  106.9 10.5 %reshape.39 = bf16[16,1,53312]{2,1,0:T(2,128)(2,1)S(1)} reshape(bf16[16,2,26656]{2,1,0:T(2,128)(2,1)} %all-to-all-done) | data formatting | bytes 3411968
  117.4 5.2 %convert_reduce_fusion = f32[53312]{0:T(1024)} fusion(bf16[16,1,53312]{2,1,0:T(2,128)(2,1)S(1)} %reshape.39), kind=kLoop, calls=%fused_computation | loop fusion | flops 1652672 | bytes 1919232 | tf_op jit(solution)/shard_map/reduce_sum | solution.py:23
  122.6 1.8 reshape.22
  124.5 1.7 convolution_reduce_fusion
  126.3 2.1 convolution_bitcast_fusion.1
  128.3 24.0 %all-reduce.8.cloned.1.call-done = f32[2,26656]{1,0:T(2,128)} async-done(((f32[2,26656]{1,0:T(2,128)}), f32[2,26656]{1,0:T(2,128)}) %all-reduce.8.cloned.1.call-update) | async-done | bytes 213264
  152.3 2.0 fusion
  154.4 1.1 convolution_bitcast_fusion
  155.5 39.4 %all-reduce.2 = (f32[6]{0:T(128)S(1)}, f32[6]{0:T(128)S(1)}) all-reduce(f32[6]{0:T(128)S(1)} %convolution_bitcast_fusion, f32[6]{0:T(128)S(1)} %convolution_bitcast_fusion.1), channel_id=1, replica_groups=mesh['replica'=16,'spatial'=2] {'replica','spatial'}, use_global_device_ids=true, to_apply=%region_3.0 | all-reduce | flops 12 | bytes 96 | tf_op jit(solution)/shard_map/psum | solution.py:30
  194.9 0.8 convolution_reduce_fusion.1
  195.8 0.7 fusion.22
  196.6 0.6 dynamic-update-slice
  197.2 1.2 copy-done
  198.4 133.0 %all-reduce.6.cloned.1.call-done = bf16[852992]{0:T(1024)(128)(2,1)} async-done(((bf16[852992]{0:T(1024)(128)(2,1)}), bf16[852992]{0:T(1024)(128)(2,1)}) %all-reduce.6.cloned.1.call-update) | async-done | bytes 1706000
  331.5 2.7 copy.13
  (25 shorter events, 0.9 us)
Async XLA Ops:
  65.0 7.7 %copy-start.1 = (f32[26656]{0:T(1024)S(1)}, f32[26656]{0:T(1024)}, u32[]{:S(2)}) copy-start(f32[26656]{0:T(1024)} %param.7) | copy-start | bytes 319876
  65.0 8.4 %copy-start.4 = (s32[6]{0:T(128)S(1)}, s32[6]{0:T(128)}, u32[]{:S(2)}) copy-start(s32[6]{0:T(128)} %param.10) | copy-start | bytes 76
  65.0 8.4 %copy-start.6 = (s32[6]{0:T(128)S(1)}, s32[6]{0:T(128)}, u32[]{:S(2)}) copy-start(s32[6]{0:T(128)} %param.9) | copy-start | bytes 76
  65.0 8.4 %copy-start.7 = (u32[32]{0:T(128)S(1)}, u32[32]{0:T(128)}, u32[]{:S(2)}) copy-start(u32[32]{0:T(128)} %constant.36) | copy-start | bytes 388
  65.0 41.9 %all-to-all-start = ((bf16[16,2,26656]{2,1,0:T(2,128)(2,1)}), bf16[16,2,26656]{2,1,0:T(2,128)(2,1)}, u32[]{:S(2)}, u32[]{:S(2)}) async-start(bf16[16,2,26656]{2,1,0:T(2,128)(2,1)} %reshape.38), calls=%async_computation | async-start | bytes 3424256 | tf_op jit(solution)/shard_map/all_to_all | solution.py:16
  72.5 79.8 %all-reduce.8.cloned.1.call-start = ((), (), s32[]{:S(2)}) async-start(), calls=%async_computation.2 | async-start | bytes 428032
  117.4 7.1 %copy-start.5 = (s32[6]{0:T(128)S(1)}, s32[6]{0:T(128)}, u32[]{:S(2)}) copy-start(s32[6]{0:T(128)} %param.11) | copy-start | bytes 76
  122.6 31.8 %copy-start.3 = (s32[26656]{0:T(1024)S(1)}, s32[26656]{0:T(1024)}, u32[]{:S(2)}) copy-start(s32[26656]{0:T(1024)} %iota_add_fusion) | copy-start | bytes 319876
  124.5 207.0 %all-reduce.6.cloned.1.call-start = ((), (), s32[]{:S(2)}) async-start(), calls=%async_computation.1 | async-start | bytes 3411968
  126.2 69.5 %copy-start.2 = (f32[26656]{0:T(1024)S(1)}, f32[26656]{0:T(1024)}, u32[]{:S(2)}) copy-start(f32[26656]{0:T(1024)} %param.8) | copy-start | bytes 319876
  197.2 1.2 copy-start
Sparse Core Ops, SparseCore 0:
  124.6 27.6 all-reduce.7
  198.6 132.8 all-reduce.5
where the time goes:
time: 342 us; the launch traced here: 341 us
  waiting for transfers between devices  189 us (55%)
  other arithmetic  59.7 us (17%)
  blocking collectives  39.4 us (12%)
  local copies, waits for them, and re-layouts  25.2 us (7%)
  between operations  14.2 us (4%)
  starting transfers between devices  7.66 us (2%)
  matrix products  5.68 us (2%)
    unnamed x4, waiting for transfers between devices  157 us
    psum x1, blocking collectives, shards(): wsq, gsq = lax.psum((wsq_local, gsq_local), ('replica', 'spatial'))  39.4 us
    unnamed x1, other arithmetic  37.8 us
    all_to_all x1, waiting for transfers between devices, shards(): lax.all_to_all(grads[0, 0].reshape(n_rep, n_spa * shard), 'replica', spli...  32.2 us
    unnamed x22, local copies, waits for them, and re-layouts  19.1 us
    all_to_all x1, other arithmetic, shards(): lax.all_to_all(grads[0, 0].reshape(n_rep, n_spa * shard), 'replica', spli...  13.3 us
    all_to_all x1, starting transfers between devices, shards(): lax.all_to_all(grads[0, 0].reshape(n_rep, n_spa * shard), 'replica', spli...  7.57 us
  transfers between devices with their start and end apart: 3, of which 3 were waited for; matrix products, arithmetic and copies ran while one was open for 2% of the time, Pallas kernels for 0%

commit v1 on v0

--- a/solution.py
+++ b/solution.py
@@ -27,7 +27,7 @@
     grad = summed.reshape(shard) / (n_rep * n_spa)
     gsq_local = jnp.dot(onehot, grad * grad, precision=lax.Precision.HIGHEST)
     wsq_local = jnp.dot(onehot, master * master, precision=lax.Precision.HIGHEST)
-    wsq, gsq = lax.psum((wsq_local, gsq_local), ("replica", "spatial"))
+    wsq, gsq = lax.psum(lax.psum((wsq_local, gsq_local), "replica"), "spatial")
     wnorm = jnp.sqrt(wsq)
     gnorm = jnp.sqrt(gsq)
     skipped = lars_skip.astype(jnp.float32)

time: 342 us -> 336 us (0.982)
  waiting for transfers between devices: 189 us -> 185 us
    unnamed x4, waiting for transfers between devices: 157 us -> 153 us
    psum x1 -> x2, blocking collectives: 39.4 us -> 37.8 us  [shards(): wsq, gsq = lax.psum(lax.psum((wsq_local, gsq_local), 'replica'), 'spatial')]
where the time goes in v1:
time: 336 us; the launch traced here: 335 us
  waiting for transfers between devices  185 us (55%)
  other arithmetic  59.7 us (18%)
  blocking collectives  37.8 us (11%)
  local copies, waits for them, and re-layouts  25.2 us (8%)
  between operations  14.2 us (4%)
  starting transfers between devices  7.66 us (2%)
  matrix products  5.68 us (2%)
    unnamed x4, waiting for transfers between devices  153 us
    unnamed x1, other arithmetic  37.8 us
    psum x2, blocking collectives, shards(): wsq, gsq = lax.psum(lax.psum((wsq_local, gsq_local), 'replica'), 'spatial')  37.8 us
    all_to_all x1, waiting for transfers between devices, shards(): lax.all_to_all(grads[0, 0].reshape(n_rep, n_spa * shard), 'replica', spli...  32.2 us
    unnamed x22, local copies, waits for them, and re-layouts  19.1 us
    all_to_all x1, other arithmetic, shards(): lax.all_to_all(grads[0, 0].reshape(n_rep, n_spa * shard), 'replica', spli...  13.3 us
    all_to_all x1, starting transfers between devices, shards(): lax.all_to_all(grads[0, 0].reshape(n_rep, n_spa * shard), 'replica', spli...  7.57 us
  transfers between devices with their start and end apart: 3, of which 3 were waited for; matrix products, arithmetic and copies ran while one was open for 2% of the time, Pallas kernels for 0%

profile of v1, /device:TPU:0, one launch (start us, length us, event | category | flops | bytes accessed | tf_op | source)
XLA Modules:
  0.0 335.2 jit_solution(15092341883991221009)
XLA Ops:
  7.2 37.8 %reduce.1 = bf16[852992]{0:T(1024)(128)(2,1)} reduce(bf16[1,1,852992]{2,1,0:T(2,128)(2,1)} %param.6, bf16[]{:T(256)} %constant.38), dimensions={0,1}, to_apply=%param.6.reduce_sub_computation | reduce | bytes 3411970 | tf_op args[0]
  44.9 3.0 all_to_all.8
  48.4 13.3 %reduce.8 = bf16[16,53312]{1,0:T(8,128)(2,1)} reduce(bf16[16,1,53312]{2,1,0:T(2,128)(2,1)S(1)} %all_to_all.8, bf16[]{:T(256)} %broadcast.54), dimensions={1}, to_apply=%all_to_all.8.reduce_sub_computation | reduce | bytes 3411970 | tf_op jit(solution)/shard_map/all_to_all | solution.py:16
  61.8 3.2 reshape.38
  65.0 7.6 %all-to-all-start = ((bf16[16,2,26656]{2,1,0:T(2,128)(2,1)}), bf16[16,2,26656]{2,1,0:T(2,128)(2,1)}, u32[]{:S(2)}, u32[]{:S(2)}) async-start(bf16[16,2,26656]{2,1,0:T(2,128)(2,1)} %reshape.38), calls=%async_computation | async-start | bytes 3424256 | tf_op jit(solution)/shard_map/all_to_all | solution.py:16
  72.6 0.7 reshape.25
  73.4 0.7 dynamic-slice
  74.1 0.7 iota_add_fusion
  74.7 32.2 %all-to-all-done = bf16[16,2,26656]{2,1,0:T(2,128)(2,1)} async-done(((bf16[16,2,26656]{2,1,0:T(2,128)(2,1)}), bf16[16,2,26656]{2,1,0:T(2,128)(2,1)}, u32[]{:S(2)}, u32[]{:S(2)}) %all-to-all-start) | async-done | bytes 1706016 | tf_op jit(solution)/shard_map/all_to_all | solution.py:16
  106.9 10.5 %reshape.39 = bf16[16,1,53312]{2,1,0:T(2,128)(2,1)S(1)} reshape(bf16[16,2,26656]{2,1,0:T(2,128)(2,1)} %all-to-all-done) | data formatting | bytes 3411968
  117.4 5.2 %convert_reduce_fusion = f32[53312]{0:T(1024)} fusion(bf16[16,1,53312]{2,1,0:T(2,128)(2,1)S(1)} %reshape.39), kind=kLoop, calls=%fused_computation | loop fusion | flops 1652672 | bytes 1919232 | tf_op jit(solution)/shard_map/reduce_sum | solution.py:23
  122.6 1.8 reshape.22
  124.5 1.7 convolution_reduce_fusion
  126.3 2.1 convolution_bitcast_fusion.1
  128.3 24.0 %all-reduce.9.cloned.1.call-done = f32[2,26656]{1,0:T(2,128)} async-done(((f32[2,26656]{1,0:T(2,128)}), f32[2,26656]{1,0:T(2,128)}) %all-reduce.9.cloned.1.call-update) | async-done | bytes 213264
  152.3 2.0 fusion
  154.4 1.1 convolution_bitcast_fusion
  155.5 32.8 %all-reduce.2 = (f32[6]{0:T(128)S(1)}, f32[6]{0:T(128)S(1)}) all-reduce(f32[6]{0:T(128)S(1)} %convolution_bitcast_fusion, f32[6]{0:T(128)S(1)} %convolution_bitcast_fusion.1), channel_id=1, replica_groups=mesh['replica'=16,'spatial'=2] {'replica'}, use_global_device_ids=true, to_apply=%region_4.0 | all-reduce | flops 12 | bytes 96 | tf_op jit(solution)/shard_map/psum | solution.py:30
  188.4 4.9 %all-reduce.3 = (f32[6]{0:T(128)S(1)}, f32[6]{0:T(128)S(1)}) all-reduce(f32[6]{0:T(128)S(1)} %get-tuple-element.3, f32[6]{0:T(128)S(1)} %get-tuple-element.4), channel_id=1, replica_groups=mesh['replica'=16,'spatial'=2] {'spatial'}, use_global_device_ids=true, to_apply=%region_5.0 | all-reduce | flops 12 | bytes 96 | tf_op jit(solution)/shard_map/psum | solution.py:30
  193.3 0.8 convolution_reduce_fusion.1
  194.1 0.7 fusion.22
  195.6 1.2 copy-done
  196.8 128.8 %all-reduce.7.cloned.1.call-done = bf16[852992]{0:T(1024)(128)(2,1)} async-done(((bf16[852992]{0:T(1024)(128)(2,1)}), bf16[852992]{0:T(1024)(128)(2,1)}) %all-reduce.7.cloned.1.call-update) | async-done | bytes 1706000
  325.6 2.7 copy.13
  (26 shorter events, 1.5 us)
Async XLA Ops:
  65.0 7.7 %copy-start.1 = (f32[26656]{0:T(1024)S(1)}, f32[26656]{0:T(1024)}, u32[]{:S(2)}) copy-start(f32[26656]{0:T(1024)} %param.7) | copy-start | bytes 319876
  65.0 8.4 %copy-start.4 = (s32[6]{0:T(128)S(1)}, s32[6]{0:T(128)}, u32[]{:S(2)}) copy-start(s32[6]{0:T(128)} %param.10) | copy-start | bytes 76
  65.0 8.4 %copy-start.6 = (s32[6]{0:T(128)S(1)}, s32[6]{0:T(128)}, u32[]{:S(2)}) copy-start(s32[6]{0:T(128)} %param.9) | copy-start | bytes 76
  65.0 8.4 %copy-start.7 = (u32[32]{0:T(128)S(1)}, u32[32]{0:T(128)}, u32[]{:S(2)}) copy-start(u32[32]{0:T(128)} %constant.36) | copy-start | bytes 388
  65.0 41.9 %all-to-all-start = ((bf16[16,2,26656]{2,1,0:T(2,128)(2,1)}), bf16[16,2,26656]{2,1,0:T(2,128)(2,1)}, u32[]{:S(2)}, u32[]{:S(2)}) async-start(bf16[16,2,26656]{2,1,0:T(2,128)(2,1)} %reshape.38), calls=%async_computation | async-start | bytes 3424256 | tf_op jit(solution)/shard_map/all_to_all | solution.py:16
  72.5 79.8 %all-reduce.9.cloned.1.call-start = ((), (), s32[]{:S(2)}) async-start(), calls=%async_computation.2 | async-start | bytes 428032
  117.4 7.1 %copy-start.5 = (s32[6]{0:T(128)S(1)}, s32[6]{0:T(128)}, u32[]{:S(2)}) copy-start(s32[6]{0:T(128)} %param.11) | copy-start | bytes 76
  122.6 31.8 %copy-start.3 = (s32[26656]{0:T(1024)S(1)}, s32[26656]{0:T(1024)}, u32[]{:S(2)}) copy-start(s32[26656]{0:T(1024)} %iota_add_fusion) | copy-start | bytes 319876
  124.5 201.1 %all-reduce.7.cloned.1.call-start = ((), (), s32[]{:S(2)}) async-start(), calls=%async_computation.1 | async-start | bytes 3411968
  126.2 67.8 %copy-start.2 = (f32[26656]{0:T(1024)S(1)}, f32[26656]{0:T(1024)}, u32[]{:S(2)}) copy-start(f32[26656]{0:T(1024)} %param.8) | copy-start | bytes 319876
  195.6 1.2 copy-start
Sparse Core Ops, SparseCore 0:
  124.6 27.6 all-reduce.8
  196.9 128.6 all-reduce.6
